TPU v7x, 32 devices: a whole 2x2x4 slice. The times are simulated.
32 devices in a mesh: section: 2 (over x), lat: 4 (over y, core), lon: 4 (over z).
Axes of the slice: x: 2, y: 2, z: 4, core: 2. Of those that a mesh axis runs over, the one named last changes fastest.
Arguments:
- fields_in: bfloat16 [4, 96, 64, 512], P('section', None, 'lat', 'lon'), may hold values from -6 to 6
- plan: int32 [4], replicated, may hold values from 0 to 3, as said below
- in_proj: bfloat16 [64, 96], replicated, may hold values from -0.625 to 0.625
- enc_conv: bfloat16 [9, 64, 64], replicated, may hold values from -0.25 to 0.25
- down_conv: bfloat16 [9, 128, 64], replicated, may hold values from -0.25 to 0.25
- mid_conv: bfloat16 [9, 128, 128], replicated, may hold values from -0.1875 to 0.1875
- up_proj: bfloat16 [64, 128], replicated, may hold values from -0.5 to 0.5
- unite_conv: bfloat16 [9, 64, 128], replicated, may hold values from -0.1875 to 0.1875
- out_proj: bfloat16 [96, 64], replicated, may hold values from -0.75 to 0.75
Outputs:
- corrected: bfloat16 [4, 96, 64, 512], P('section', None, 'lat', 'lon')
Inputs may be any that keep to these rules, and one draw needn't show every extreme that they name: `plan`: each micro-batch appears once; the first turn takes one of the last 2 micro-batches and the last turn one of the first 2.
All inputs are finite; a program needn't handle non-finite values.
Results may differ from a plain program's by a relative error of at most 0.0072.
Values may be sent and summed in bfloat16 or wider, within the bound.
No kernel may reach another device: no remote copies, remote signals or barrier semaphores. Data moves between devices by JAX's collectives and lax.ppermute only.
A program may use at most 64 MiB of HBM per device.

v0:
```python
import jax
import jax.numpy as jnp
from jax import lax
from jax.sharding import PartitionSpec as P


def padded_2(block, sides, width, periodic):
    for axis, dim in sides:
        count = lax.axis_size(axis)
        forward = [(i, i + 1) for i in range(count - 1)]
        if periodic:
            forward.append((count - 1, 0))
        backward = [(target, source) for source, target in forward]
        low = lax.ppermute(
            lax.slice_in_dim(block, block.shape[dim] - width, None, axis=dim), axis, forward
        )
        high = lax.ppermute(lax.slice_in_dim(block, 0, width, axis=dim), axis, backward)
        block = jnp.concatenate([low, block, high], axis=dim)
    return block


def convolve(source, kernel):
    batch, channels, height, breadth = source.shape
    wide = padded_2(source, (("lon", 3),), 1, True)
    padded = padded_2(wide, (("lat", 2),), 1, False)
    summed = jnp.zeros((batch, kernel.shape[1], height, breadth), jnp.float32)
    for offset_row in range(3):
        for offset_col in range(3):
            window = padded[
                :, :, offset_row : offset_row + height, offset_col : offset_col + breadth
            ]
            summed = summed + jnp.einsum(
                "oc,bchw->bohw",
                kernel[3 * offset_row + offset_col],
                window,
                preferred_element_type=jnp.float32,
            )
    return summed


def encode(sample, in_proj, enc_conv, down_conv):
    batch, variables, height, breadth = sample.shape
    stem_map = jax.nn.gelu(
        jnp.einsum("cv,bvhw->bchw", in_proj, sample, preferred_element_type=jnp.float32)
    )
    stem_map = stem_map.astype(jnp.bfloat16)
    skip_map = jax.nn.gelu(convolve(stem_map, enc_conv)).astype(jnp.bfloat16)
    pooled = (
        skip_map.astype(jnp.float32)
        .reshape(batch, -1, height // 2, 2, breadth // 2, 2)
        .mean(axis=(3, 5))
        .astype(jnp.bfloat16)
    )
    deep_map = jax.nn.gelu(convolve(pooled, down_conv)).astype(jnp.bfloat16)
    return (skip_map, deep_map)


def decode(skip_map, deep_map, mid_conv, up_proj, unite_conv, out_proj):
    middle = (jax.nn.gelu(convolve(deep_map, mid_conv)) + deep_map.astype(jnp.float32)).astype(
        jnp.bfloat16
    )
    lifted = jnp.einsum(
        "oc,bchw->bohw", up_proj, middle, preferred_element_type=jnp.float32
    ).astype(jnp.bfloat16)
    enlarged = jnp.repeat(jnp.repeat(lifted, 2, axis=2), 2, axis=3)
    joined = jnp.concatenate([enlarged, skip_map], axis=1)
    merged = jax.nn.gelu(convolve(joined, unite_conv)).astype(jnp.bfloat16)
    result = jnp.einsum("oc,bchw->bohw", out_proj, merged, preferred_element_type=jnp.float32)
    return result.astype(jnp.bfloat16)


def shards(fields_in, plan, in_proj, enc_conv, down_conv, mid_conv, up_proj, unite_conv, out_proj):
    per_section = fields_in.shape[0]
    section_index = lax.axis_index("section")
    gathered = lax.all_gather(fields_in, "section", axis=0, tiled=True)
    picked = []
    for local_num in range(per_section):
        tick_num = section_index * per_section + local_num
        picked.append(lax.dynamic_index_in_dim(gathered, plan[tick_num], 0, keepdims=True))
    samples = jnp.concatenate(picked, axis=0)
    skip_map, deep_map = encode(samples, in_proj, enc_conv, down_conv)
    return decode(skip_map, deep_map, mid_conv, up_proj, unite_conv, out_proj)


def solution(mesh):
    return jax.shard_map(
        shards,
        mesh=mesh,
        in_specs=(P("section", None, "lat", "lon"), P(), P(), P(), P(), P(), P(), P(), P()),
        out_specs=P("section", None, "lat", "lon"),
        check_vma=False,
    )
```

profile of v0, /device:TPU:1, one launch (start us, length us, event | category | flops | bytes accessed | tf_op | source)
XLA Modules:
  0.0 157.2 jit_solution(12778346985313081739)
XLA Ops:
  6.5 0.7 all-gather.2.cloned.1.call-update
  7.3 1.4 fusion.249
  12.6 25.4 %all-gather.2.cloned.1.call-done = bf16[4,96,16,128]{3,2,1,0:T(8,128)(2,1)} async-done(((bf16[2,96,16,128]{3,2,1,0:T(8,128)(2,1)}), bf16[4,96,16,128]{3,2,1,0:T(8,128)(2,1)}) %all-gather.2.cloned.1.call-update) | async-done | bytes 1572880 | tf_op jit(solution)/shard_map/all_gather | solution.py:75
  38.0 1.2 constant_dynamic-slice_fusion.1
  39.5 0.5 fusion.40
  40.2 1.3 collective-permute-start
  41.5 2.1 %collective-permute-start.1 = (bf16[2,64,16,1]{3,1,2,0:T(8,128)(2,1)S(1)}, bf16[2,64,16,1]{3,1,2,0:T(8,128)(2,1)S(1)}, u32[]{:S(2)}, u32[]{:S(2)}) collective-permute-start(bf16[2,64,16,1]{3,1,2,0:T(8,128)(2,1)S(1)} %get-tuple-element.18), channel_id=1, source_target_pairs={{1,0},{2,1},{3,2},{0,3},{5,4},{6,5},{7,6},{4,7},{9,8},{10,9},{11,1... | collective-permute-start | bytes 12296 | tf_op jit(solution)/shard_map/ppermute | solution.py:17
  43.9 10.9 %collective-permute-done = bf16[2,64,16,1]{3,1,2,0:T(8,128)(2,1)S(1)} collective-permute-done((bf16[2,64,16,1]{3,1,2,0:T(8,128)(2,1)S(1)}, bf16[2,64,16,1]{3,1,2,0:T(8,128)(2,1)S(1)}, u32[]{:S(2)}, u32[]{:S(2)}) %collective-permute-start) | collective-permute-done | bytes 4128 | tf_op jit(solution)/shard_map/ppermute | solution.py:14
  54.8 11.2 %collective-permute-done.1 = bf16[2,64,16,1]{3,1,2,0:T(8,128)(2,1)S(1)} collective-permute-done((bf16[2,64,16,1]{3,1,2,0:T(8,128)(2,1)S(1)}, bf16[2,64,16,1]{3,1,2,0:T(8,128)(2,1)S(1)}, u32[]{:S(2)}, u32[]{:S(2)}) %collective-permute-start.1) | collective-permute-done | bytes 4128 | tf_op jit(solution)/shard_map/ppermute | solution.py:17
  66.1 4.1 %collective-permute-start.2 = (bf16[2,64,1,130]{3,1,2,0:T(8,128)(2,1)S(1)}, bf16[2,64,1,130]{3,1,2,0:T(8,128)(2,1)S(1)}, u32[]{:S(2)}, u32[]{:S(2)}) collective-permute-start(bf16[2,64,1,130]{3,1,2,0:T(8,128)(2,1)S(1)} %get-tuple-element.11), channel_id=1, source_target_pairs={{0,4},{4,8},{8,12},{1,5},{5,9},{9,13},{2,6},{6,10},{10,14},{3,7},{... | collective-permute-start | bytes 99848 | tf_op jit(solution)/shard_map/ppermute | solution.py:14
  70.2 1.9 %collective-permute-start.3 = (bf16[2,64,1,130]{3,1,2,0:T(8,128)(2,1)S(1)}, bf16[2,64,1,130]{3,1,2,0:T(8,128)(2,1)S(1)}, u32[]{:S(2)}, u32[]{:S(2)}) collective-permute-start(bf16[2,64,1,130]{3,1,2,0:T(8,128)(2,1)S(1)} %get-tuple-element.12), channel_id=1, source_target_pairs={{4,0},{8,4},{12,8},{5,1},{9,5},{13,9},{6,2},{10,6},{14,10},{7,3},{... | collective-permute-start | bytes 99848 | tf_op jit(solution)/shard_map/ppermute | solution.py:17
  72.6 3.2 %collective-permute-done.3 = bf16[2,64,1,130]{3,1,2,0:T(8,128)(2,1)S(1)} collective-permute-done((bf16[2,64,1,130]{3,1,2,0:T(8,128)(2,1)S(1)}, bf16[2,64,1,130]{3,1,2,0:T(8,128)(2,1)S(1)}, u32[]{:S(2)}, u32[]{:S(2)}) %collective-permute-start.3) | collective-permute-done | bytes 33312 | tf_op jit(solution)/shard_map/ppermute | solution.py:17
  75.8 1.0 maximum_maximum_fusion.1
  79.0 0.9 fusion.48
  80.2 1.7 %reduce_sum.9 = f32[2,64,8,64]{1,3,2,0:T(8,128)S(1)} reduce(f32[2,64,8,2,64,2]{1,5,4,3,2,0:T(2,128)S(1)} %bitcast.317, f32[]{:T(128)} %constant.37.clone.1), dimensions={3,5}, to_apply=%region_0.1 | reduce | flops 196608 | bytes 1310724 | tf_op jit(solution)/shard_map/reduce_sum | solution.py:51
  82.0 0.9 collective-permute-start.4
  83.0 2.4 %collective-permute-start.5 = (bf16[2,64,8,1]{1,3,2,0:T(2,128)(2,1)S(1)}, bf16[2,64,8,1]{1,3,2,0:T(2,128)(2,1)S(1)}, u32[]{:S(2)}, u32[]{:S(2)}) collective-permute-start(bf16[2,64,8,1]{1,3,2,0:T(2,128)(2,1)S(1)} %get-tuple-element.30), channel_id=1, source_target_pairs={{1,0},{2,1},{3,2},{0,3},{5,4},{6,5},{7,6},{4,7},{9,8},{10,9},{11,1... | collective-permute-start | bytes 6152 | tf_op jit(solution)/shard_map/ppermute | solution.py:17
  85.6 0.8 collective-permute-done.4
  86.4 3.0 %collective-permute-start.6 = (bf16[2,64,1,66]{1,3,2,0:T(8,128)(2,1)S(1)}, bf16[2,64,1,66]{1,3,2,0:T(8,128)(2,1)S(1)}, u32[]{:S(2)}, u32[]{:S(2)}) collective-permute-start(bf16[2,64,1,66]{1,3,2,0:T(8,128)(2,1)S(1)} %get-tuple-element.25), channel_id=1, source_target_pairs={{0,4},{4,8},{8,12},{1,5},{5,9},{9,13},{2,6},{6,10},{10,14},{3,7},{... | collective-permute-start | bytes 50696 | tf_op jit(solution)/shard_map/ppermute | solution.py:14
  89.4 1.9 %collective-permute-start.7 = (bf16[2,64,1,66]{1,3,2,0:T(8,128)(2,1)S(1)}, bf16[2,64,1,66]{1,3,2,0:T(8,128)(2,1)S(1)}, u32[]{:S(2)}, u32[]{:S(2)}) collective-permute-start(bf16[2,64,1,66]{1,3,2,0:T(8,128)(2,1)S(1)} %get-tuple-element.26), channel_id=1, source_target_pairs={{4,0},{8,4},{12,8},{5,1},{9,5},{13,9},{6,2},{10,6},{14,10},{7,3},{... | collective-permute-start | bytes 50696 | tf_op jit(solution)/shard_map/ppermute | solution.py:17
  91.6 3.1 %collective-permute-done.7 = bf16[2,64,1,66]{1,3,2,0:T(8,128)(2,1)S(1)} collective-permute-done((bf16[2,64,1,66]{1,3,2,0:T(8,128)(2,1)S(1)}, bf16[2,64,1,66]{1,3,2,0:T(8,128)(2,1)S(1)}, u32[]{:S(2)}, u32[]{:S(2)}) %collective-permute-start.7) | collective-permute-done | bytes 16928 | tf_op jit(solution)/shard_map/ppermute | solution.py:17
  96.0 1.0 fusion.17
  96.9 1.1 fusion.82
  98.2 3.6 %collective-permute-start.9 = (bf16[2,128,8,1]{1,3,2,0:T(2,128)(2,1)S(1)}, bf16[2,128,8,1]{1,3,2,0:T(2,128)(2,1)S(1)}, u32[]{:S(2)}, u32[]{:S(2)}) collective-permute-start(bf16[2,128,8,1]{1,3,2,0:T(2,128)(2,1)S(1)} %get-tuple-element.28), channel_id=1, source_target_pairs={{1,0},{2,1},{3,2},{0,3},{5,4},{6,5},{7,6},{4,7},{9,8},{10,9},{11,1... | collective-permute-start | bytes 12296 | tf_op jit(solution)/shard_map/ppermute | solution.py:17
  102.0 0.8 collective-permute-done.8
  102.8 2.7 %collective-permute-start.10 = (bf16[2,128,1,66]{1,3,2,0:T(8,128)(2,1)S(1)}, bf16[2,128,1,66]{1,3,2,0:T(8,128)(2,1)S(1)}, u32[]{:S(2)}, u32[]{:S(2)}) collective-permute-start(bf16[2,128,1,66]{1,3,2,0:T(8,128)(2,1)S(1)} %get-tuple-element.21), channel_id=1, source_target_pairs={{0,4},{4,8},{8,12},{1,5},{5,9},{9,13},{2,6},{6,10},{10,14},{3,7},{... | collective-permute-start | bytes 101384 | tf_op jit(solution)/shard_map/ppermute | solution.py:14
  105.5 2.1 %collective-permute-start.11 = (bf16[2,128,1,66]{1,3,2,0:T(8,128)(2,1)S(1)}, bf16[2,128,1,66]{1,3,2,0:T(8,128)(2,1)S(1)}, u32[]{:S(2)}, u32[]{:S(2)}) collective-permute-start(bf16[2,128,1,66]{1,3,2,0:T(8,128)(2,1)S(1)} %get-tuple-element.22), channel_id=1, source_target_pairs={{4,0},{8,4},{12,8},{5,1},{9,5},{13,9},{6,2},{10,6},{14,10},{7,3},{... | collective-permute-start | bytes 101384 | tf_op jit(solution)/shard_map/ppermute | solution.py:17
  107.9 2.9 %collective-permute-done.11 = bf16[2,128,1,66]{1,3,2,0:T(8,128)(2,1)S(1)} collective-permute-done((bf16[2,128,1,66]{1,3,2,0:T(8,128)(2,1)S(1)}, bf16[2,128,1,66]{1,3,2,0:T(8,128)(2,1)S(1)}, u32[]{:S(2)}, u32[]{:S(2)}) %collective-permute-start.11) | collective-permute-done | bytes 33824 | tf_op jit(solution)/shard_map/ppermute | solution.py:17
  112.4 0.6 fusion.29
  113.7 0.9 copy.22
  115.8 3.6 %collective-permute-start.13 = (bf16[2,128,16,1]{1,2,3,0:T(8,128)(2,1)S(1)}, bf16[2,128,16,1]{1,2,3,0:T(8,128)(2,1)S(1)}, u32[]{:S(2)}, u32[]{:S(2)}) collective-permute-start(bf16[2,128,16,1]{1,2,3,0:T(8,128)(2,1)S(1)} %copy.24), channel_id=1, source_target_pairs={{1,0},{2,1},{3,2},{0,3},{5,4},{6,5},{7,6},{4,7},{9,8},{10,9},{11,1... | collective-permute-start | bytes 24584 | tf_op jit(solution)/shard_map/ppermute | solution.py:17
  119.5 1.3 fusion.32
  120.7 3.0 %collective-permute-done.12 = bf16[2,128,16,1]{1,2,3,0:T(8,128)(2,1)S(1)} collective-permute-done((bf16[2,128,16,1]{1,2,3,0:T(8,128)(2,1)S(1)}, bf16[2,128,16,1]{1,2,3,0:T(8,128)(2,1)S(1)}, u32[]{:S(2)}, u32[]{:S(2)}) %collective-permute-start.12) | collective-permute-done | bytes 8224 | tf_op jit(solution)/shard_map/ppermute | solution.py:14
  123.8 0.5 copy.25
  124.3 0.5 copy.26
  125.0 3.3 %collective-permute-start.14 = (bf16[2,128,1,130]{3,1,2,0:T(8,128)(2,1)S(1)}, bf16[2,128,1,130]{3,1,2,0:T(8,128)(2,1)S(1)}, u32[]{:S(2)}, u32[]{:S(2)}) collective-permute-start(bf16[2,128,1,130]{3,1,2,0:T(8,128)(2,1)S(1)} %get-tuple-element.7), channel_id=1, source_target_pairs={{0,4},{4,8},{8,12},{1,5},{5,9},{9,13},{2,6},{6,10},{10,14},{3,7},{... | collective-permute-start | bytes 199688 | tf_op jit(solution)/shard_map/ppermute | solution.py:14
  128.3 1.9 %collective-permute-start.15 = (bf16[2,128,1,130]{3,1,2,0:T(8,128)(2,1)S(1)}, bf16[2,128,1,130]{3,1,2,0:T(8,128)(2,1)S(1)}, u32[]{:S(2)}, u32[]{:S(2)}) collective-permute-start(bf16[2,128,1,130]{3,1,2,0:T(8,128)(2,1)S(1)} %get-tuple-element.8), channel_id=1, source_target_pairs={{4,0},{8,4},{12,8},{5,1},{9,5},{13,9},{6,2},{10,6},{14,10},{7,3},{... | collective-permute-start | bytes 199688 | tf_op jit(solution)/shard_map/ppermute | solution.py:17
  130.2 0.7 fusion.65
  130.9 3.7 %collective-permute-done.15 = bf16[2,128,1,130]{3,1,2,0:T(8,128)(2,1)S(1)} collective-permute-done((bf16[2,128,1,130]{3,1,2,0:T(8,128)(2,1)S(1)}, bf16[2,128,1,130]{3,1,2,0:T(8,128)(2,1)S(1)}, u32[]{:S(2)}, u32[]{:S(2)}) %collective-permute-start.15) | collective-permute-done | bytes 66592 | tf_op jit(solution)/shard_map/ppermute | solution.py:17
  134.6 3.2 %maximum_maximum_fusion = (bf16[2,128,17,130]{3,1,2,0:T(8,128)(2,1)S(1)}, bf16[2,128,17,130]{3,1,2,0:T(8,128)(2,1)S(1)}) fusion(bf16[2,128,16,1]{3,1,2,0:T(8,128)(2,1)S(1)} %copy.26, bf16[2,64,16,128]{3,1,2,0:T(8,128)(2,1)S(1)} %fusion.48, bf16[2,64,16,128]{3,1,2,0:T(8,128)(2,1)S(1)} %copy.22, bf16[2,128,16,1]{3,1,2,0:T(8,128)(2,1)S(1)} %copy.25, ...), kind=kLoop, calls=%fused_computation | loop fusion | flops 11315200 | bytes 3461120 | tf_op jit(solution)/shard_map/concatenate | solution.py:18
  137.8 0.6 fusion.67
  138.4 0.6 fusion.69
  139.0 0.6 fusion.57
  139.5 1.5 fusion.59
  141.1 1.3 fusion.61
  142.4 1.4 fusion.6
  143.8 4.2 %fusion.14 = bf16[2,96,16,128]{3,1,2,0:T(8,128)(2,1)} fusion(f32[2,16,128,64]{2,3,1,0:T(8,128)S(1)} %fusion.57, f32[2,16,128,64]{2,3,1,0:T(8,128)} %fusion.59, f32[2,16,128,64]{2,3,1,0:T(8,128)} %fusion.61, f32[2,16,128,64]{2,3,1,0:T(8,128)} %fusion.6, bf16[2,128,16,1]{3,1,2,0:T(8,128)(2,1)S(1)} %copy.26, bf16[2,64,16,128]{3,1,2,0:T(8,128)(2,1)S(1)} %fusion.48, ...), kind=kOutput, calls=%fused_computation.30 | convolution fusion | flops 124387328 | bytes 7110656 | tf_op jit(solution)/shard_map/oc,bchw->bohw/dot_general | solution.py:68
  148.0 2.3 %copy.29 = bf16[2,96,16,128]{3,2,1,0:T(8,128)(2,1)} copy(bf16[2,96,16,128]{3,1,2,0:T(8,128)(2,1)} %fusion.14) | data formatting | bytes 1572864 | tf_op jit(solution)/shard_map/convert_element_type | solution.py:69
  (68 shorter events, 9.9 us)
Async XLA Ops:
  6.5 137.2 %copy-start = (bf16[96,64]{0,1:T(8,128)(2,1)S(1)}, bf16[96,64]{0,1:T(8,128)(2,1)}, u32[]{:S(2)}) copy-start(bf16[96,64]{0,1:T(8,128)(2,1)} %param.17) | copy-start | bytes 36868
  6.5 32.9 %copy-start.7 = (bf16[64,96]{1,0:T(8,128)(2,1)S(1)}, bf16[64,96]{1,0:T(8,128)(2,1)}, u32[]{:S(2)}) copy-start(bf16[64,96]{1,0:T(8,128)(2,1)} %param.11) | copy-start | bytes 36868
  6.5 31.5 %all-gather.2.cloned.1.call-start = ((), (), s32[]{:S(2)}) async-start(), calls=%async_computation | async-start | bytes 2359296 | tf_op jit(solution)/shard_map/all_gather | solution.py:75
  39.5 4.1 %copy-start.3 = (bf16[9,64,64]{2,1,0:T(8,128)(2,1)S(1)}, bf16[9,64,64]{2,1,0:T(8,128)(2,1)}, u32[]{:S(2)}) copy-start(bf16[9,64,64]{2,1,0:T(8,128)(2,1)} %param.12) | copy-start | bytes 221188
  40.2 14.5 %collective-permute-start = (bf16[2,64,16,1]{3,1,2,0:T(8,128)(2,1)S(1)}, bf16[2,64,16,1]{3,1,2,0:T(8,128)(2,1)S(1)}, u32[]{:S(2)}, u32[]{:S(2)}) collective-permute-start(bf16[2,64,16,1]{3,1,2,0:T(8,128)(2,1)S(1)} %get-tuple-element.17), channel_id=1, source_target_pairs={{0,1},{1,2},{2,3},{3,0},{4,5},{5,6},{6,7},{7,4},{8,9},{9,10},{10,1... | collective-permute-start | bytes 12296 | tf_op jit(solution)/shard_map/ppermute | solution.py:14
  41.5 24.5 %collective-permute-start.1 = (bf16[2,64,16,1]{3,1,2,0:T(8,128)(2,1)S(1)}, bf16[2,64,16,1]{3,1,2,0:T(8,128)(2,1)S(1)}, u32[]{:S(2)}, u32[]{:S(2)}) collective-permute-start(bf16[2,64,16,1]{3,1,2,0:T(8,128)(2,1)S(1)} %get-tuple-element.18), channel_id=1, source_target_pairs={{1,0},{2,1},{3,2},{0,3},{5,4},{6,5},{7,6},{4,7},{9,8},{10,9},{11,1... | collective-permute-start | bytes 12296 | tf_op jit(solution)/shard_map/ppermute | solution.py:17
  66.1 6.4 %collective-permute-start.2 = (bf16[2,64,1,130]{3,1,2,0:T(8,128)(2,1)S(1)}, bf16[2,64,1,130]{3,1,2,0:T(8,128)(2,1)S(1)}, u32[]{:S(2)}, u32[]{:S(2)}) collective-permute-start(bf16[2,64,1,130]{3,1,2,0:T(8,128)(2,1)S(1)} %get-tuple-element.11), channel_id=1, source_target_pairs={{0,4},{4,8},{8,12},{1,5},{5,9},{9,13},{2,6},{6,10},{10,14},{3,7},{... | collective-permute-start | bytes 99848 | tf_op jit(solution)/shard_map/ppermute | solution.py:14
  70.2 5.6 %collective-permute-start.3 = (bf16[2,64,1,130]{3,1,2,0:T(8,128)(2,1)S(1)}, bf16[2,64,1,130]{3,1,2,0:T(8,128)(2,1)S(1)}, u32[]{:S(2)}, u32[]{:S(2)}) collective-permute-start(bf16[2,64,1,130]{3,1,2,0:T(8,128)(2,1)S(1)} %get-tuple-element.12), channel_id=1, source_target_pairs={{4,0},{8,4},{12,8},{5,1},{9,5},{13,9},{6,2},{10,6},{14,10},{7,3},{... | collective-permute-start | bytes 99848 | tf_op jit(solution)/shard_map/ppermute | solution.py:17
  80.2 5.1 %copy-start.5 = (bf16[9,128,64]{1,2,0:T(8,128)(2,1)S(1)}, bf16[9,128,64]{1,2,0:T(8,128)(2,1)}, u32[]{:S(2)}) copy-start(bf16[9,128,64]{1,2,0:T(8,128)(2,1)} %param.13) | copy-start | bytes 442372
  82.0 4.4 %collective-permute-start.4 = (bf16[2,64,8,1]{1,3,2,0:T(2,128)(2,1)S(1)}, bf16[2,64,8,1]{1,3,2,0:T(2,128)(2,1)S(1)}, u32[]{:S(2)}, u32[]{:S(2)}) collective-permute-start(bf16[2,64,8,1]{1,3,2,0:T(2,128)(2,1)S(1)} %get-tuple-element.29), channel_id=1, source_target_pairs={{0,1},{1,2},{2,3},{3,0},{4,5},{5,6},{6,7},{7,4},{8,9},{9,10},{10,1... | collective-permute-start | bytes 6152 | tf_op jit(solution)/shard_map/ppermute | solution.py:14
  83.0 3.4 %collective-permute-start.5 = (bf16[2,64,8,1]{1,3,2,0:T(2,128)(2,1)S(1)}, bf16[2,64,8,1]{1,3,2,0:T(2,128)(2,1)S(1)}, u32[]{:S(2)}, u32[]{:S(2)}) collective-permute-start(bf16[2,64,8,1]{1,3,2,0:T(2,128)(2,1)S(1)} %get-tuple-element.30), channel_id=1, source_target_pairs={{1,0},{2,1},{3,2},{0,3},{5,4},{6,5},{7,6},{4,7},{9,8},{10,9},{11,1... | collective-permute-start | bytes 6152 | tf_op jit(solution)/shard_map/ppermute | solution.py:17
  86.4 5.2 %collective-permute-start.6 = (bf16[2,64,1,66]{1,3,2,0:T(8,128)(2,1)S(1)}, bf16[2,64,1,66]{1,3,2,0:T(8,128)(2,1)S(1)}, u32[]{:S(2)}, u32[]{:S(2)}) collective-permute-start(bf16[2,64,1,66]{1,3,2,0:T(8,128)(2,1)S(1)} %get-tuple-element.25), channel_id=1, source_target_pairs={{0,4},{4,8},{8,12},{1,5},{5,9},{9,13},{2,6},{6,10},{10,14},{3,7},{... | collective-permute-start | bytes 50696 | tf_op jit(solution)/shard_map/ppermute | solution.py:14
  89.4 5.3 %collective-permute-start.7 = (bf16[2,64,1,66]{1,3,2,0:T(8,128)(2,1)S(1)}, bf16[2,64,1,66]{1,3,2,0:T(8,128)(2,1)S(1)}, u32[]{:S(2)}, u32[]{:S(2)}) collective-permute-start(bf16[2,64,1,66]{1,3,2,0:T(8,128)(2,1)S(1)} %get-tuple-element.26), channel_id=1, source_target_pairs={{4,0},{8,4},{12,8},{5,1},{9,5},{13,9},{6,2},{10,6},{14,10},{7,3},{... | collective-permute-start | bytes 50696 | tf_op jit(solution)/shard_map/ppermute | solution.py:17
  95.9 5.8 %copy-start.2 = (bf16[9,128,128]{2,1,0:T(8,128)(2,1)S(1)}, bf16[9,128,128]{2,1,0:T(8,128)(2,1)}, u32[]{:S(2)}) copy-start(bf16[9,128,128]{2,1,0:T(8,128)(2,1)} %param.14) | copy-start | bytes 884740
  98.1 4.7 %collective-permute-start.8 = (bf16[2,128,8,1]{1,3,2,0:T(2,128)(2,1)S(1)}, bf16[2,128,8,1]{1,3,2,0:T(2,128)(2,1)S(1)}, u32[]{:S(2)}, u32[]{:S(2)}) collective-permute-start(bf16[2,128,8,1]{1,3,2,0:T(2,128)(2,1)S(1)} %get-tuple-element.27), channel_id=1, source_target_pairs={{0,1},{1,2},{2,3},{3,0},{4,5},{5,6},{6,7},{7,4},{8,9},{9,10},{10,1... | collective-permute-start | bytes 12296 | tf_op jit(solution)/shard_map/ppermute | solution.py:14
  98.2 4.6 %collective-permute-start.9 = (bf16[2,128,8,1]{1,3,2,0:T(2,128)(2,1)S(1)}, bf16[2,128,8,1]{1,3,2,0:T(2,128)(2,1)S(1)}, u32[]{:S(2)}, u32[]{:S(2)}) collective-permute-start(bf16[2,128,8,1]{1,3,2,0:T(2,128)(2,1)S(1)} %get-tuple-element.28), channel_id=1, source_target_pairs={{1,0},{2,1},{3,2},{0,3},{5,4},{6,5},{7,6},{4,7},{9,8},{10,9},{11,1... | collective-permute-start | bytes 12296 | tf_op jit(solution)/shard_map/ppermute | solution.py:17
  102.8 5.1 %collective-permute-start.10 = (bf16[2,128,1,66]{1,3,2,0:T(8,128)(2,1)S(1)}, bf16[2,128,1,66]{1,3,2,0:T(8,128)(2,1)S(1)}, u32[]{:S(2)}, u32[]{:S(2)}) collective-permute-start(bf16[2,128,1,66]{1,3,2,0:T(8,128)(2,1)S(1)} %get-tuple-element.21), channel_id=1, source_target_pairs={{0,4},{4,8},{8,12},{1,5},{5,9},{9,13},{2,6},{6,10},{10,14},{3,7},{... | collective-permute-start | bytes 101384 | tf_op jit(solution)/shard_map/ppermute | solution.py:14
  105.5 5.3 %collective-permute-start.11 = (bf16[2,128,1,66]{1,3,2,0:T(8,128)(2,1)S(1)}, bf16[2,128,1,66]{1,3,2,0:T(8,128)(2,1)S(1)}, u32[]{:S(2)}, u32[]{:S(2)}) collective-permute-start(bf16[2,128,1,66]{1,3,2,0:T(8,128)(2,1)S(1)} %get-tuple-element.22), channel_id=1, source_target_pairs={{4,0},{8,4},{12,8},{5,1},{9,5},{13,9},{6,2},{10,6},{14,10},{7,3},{... | collective-permute-start | bytes 101384 | tf_op jit(solution)/shard_map/ppermute | solution.py:17
  111.7 0.7 copy-start.6
  114.6 4.9 %copy-start.4 = (bf16[9,64,128]{2,1,0:T(8,128)(2,1)S(1)}, bf16[9,64,128]{2,1,0:T(8,128)(2,1)}, u32[]{:S(2)}) copy-start(bf16[9,64,128]{2,1,0:T(8,128)(2,1)} %param.16) | copy-start | bytes 442372
  115.8 8.4 %collective-permute-start.13 = (bf16[2,128,16,1]{1,2,3,0:T(8,128)(2,1)S(1)}, bf16[2,128,16,1]{1,2,3,0:T(8,128)(2,1)S(1)}, u32[]{:S(2)}, u32[]{:S(2)}) collective-permute-start(bf16[2,128,16,1]{1,2,3,0:T(8,128)(2,1)S(1)} %copy.24), channel_id=1, source_target_pairs={{1,0},{2,1},{3,2},{0,3},{5,4},{6,5},{7,6},{4,7},{9,8},{10,9},{11,1... | collective-permute-start | bytes 24584 | tf_op jit(solution)/shard_map/ppermute | solution.py:17
  119.5 4.3 %collective-permute-start.12 = (bf16[2,128,16,1]{1,2,3,0:T(8,128)(2,1)S(1)}, bf16[2,128,16,1]{1,2,3,0:T(8,128)(2,1)S(1)}, u32[]{:S(2)}, u32[]{:S(2)}) collective-permute-start(bf16[2,128,16,1]{1,2,3,0:T(8,128)(2,1)S(1)} %copy.23), channel_id=1, source_target_pairs={{0,1},{1,2},{2,3},{3,0},{4,5},{5,6},{6,7},{7,4},{8,9},{9,10},{10,1... | collective-permute-start | bytes 24584 | tf_op jit(solution)/shard_map/ppermute | solution.py:14
  125.0 5.9 %collective-permute-start.14 = (bf16[2,128,1,130]{3,1,2,0:T(8,128)(2,1)S(1)}, bf16[2,128,1,130]{3,1,2,0:T(8,128)(2,1)S(1)}, u32[]{:S(2)}, u32[]{:S(2)}) collective-permute-start(bf16[2,128,1,130]{3,1,2,0:T(8,128)(2,1)S(1)} %get-tuple-element.7), channel_id=1, source_target_pairs={{0,4},{4,8},{8,12},{1,5},{5,9},{9,13},{2,6},{6,10},{10,14},{3,7},{... | collective-permute-start | bytes 199688 | tf_op jit(solution)/shard_map/ppermute | solution.py:14
  128.3 6.3 %collective-permute-start.15 = (bf16[2,128,1,130]{3,1,2,0:T(8,128)(2,1)S(1)}, bf16[2,128,1,130]{3,1,2,0:T(8,128)(2,1)S(1)}, u32[]{:S(2)}, u32[]{:S(2)}) collective-permute-start(bf16[2,128,1,130]{3,1,2,0:T(8,128)(2,1)S(1)} %get-tuple-element.8), channel_id=1, source_target_pairs={{4,0},{8,4},{12,8},{5,1},{9,5},{13,9},{6,2},{10,6},{14,10},{7,3},{... | collective-permute-start | bytes 199688 | tf_op jit(solution)/shard_map/ppermute | solution.py:17
  139.5 2.8 %copy-start.1 = (f32[2,16,128,64]{2,3,1,0:T(8,128)S(1)}, f32[2,16,128,64]{2,3,1,0:T(8,128)}, u32[]{:S(2)}) copy-start(f32[2,16,128,64]{2,3,1,0:T(8,128)} %fusion.32) | copy-start | bytes 3145732
Sparse Core Ops, SparseCore 0:
  8.9 29.0 all-gather.1
where the time goes:
time: 158 us; the launch traced here: 157 us
  waiting for transfers between devices  65.8 us (42%)
  starting transfers between devices  34.9 us (22%)
  matrix products  22.3 us (14%)
  between operations  17.8 us (11%)
  local copies, waits for them, and re-layouts  9.19 us (6%)
  other arithmetic  7.1 us (4%)
    all_gather x1, waiting for transfers between devices, shards(): gathered = lax.all_gather(fields_in, 'section', axis=0, tiled=True)  25.4 us
    ppermute x8, waiting for transfers between devices, padded_2(): lax.ppermute(lax.slice_in_dim(block, 0, width, axis=dim), axis, backward)  24.2 us
    ppermute x8, starting transfers between devices, padded_2(): lax.ppermute(lax.slice_in_dim(block, 0, width, axis=dim), axis, backward)  19.5 us
    dot_general x34, matrix products, convolve(): jnp.einsum('oc,bchw->bohw', kernel[3 * offset_row + offset_col], window,...  17 us
    ppermute x8, waiting for transfers between devices, padded_2(): lax.ppermute(lax.slice_in_dim(block, block.shape[dim] - width, None, axis...  15.6 us
    ppermute x8, starting transfers between devices, padded_2(): lax.ppermute(lax.slice_in_dim(block, block.shape[dim] - width, None, axis...  15.4 us
    concatenate x4, other arithmetic, padded_2(): block = jnp.concatenate([low, block, high], axis=dim)  4.52 us
    dot_general x1, matrix products, decode(): jnp.einsum('oc,bchw->bohw', out_proj, merged, preferred_element_type=jnp....  4.21 us
  transfers between devices with their start and end apart: 17, of which 10 were waited for; matrix products, arithmetic and copies ran while one was open for 3% of the time, Pallas kernels for 0%

commit v1 on v0

v1 whole, which is shorter than its diff:
```python
import jax
import jax.numpy as jnp
from jax import lax
from jax.experimental import pallas as pl
from jax.experimental.pallas import tpu as pltpu
from jax.sharding import PartitionSpec as P

BF = jnp.bfloat16
F32 = jnp.float32
HALO = 8


def gelu(x):
    inner = x * (0.7978845608028654 + 0.035677408136300125 * (x * x))
    half = 0.5 * x
    return half + half * jnp.tanh(inner)


def dot(a, b):
    return jnp.dot(a, b, preferred_element_type=F32)


def shift(x, by):
    n = x.shape[1]
    by = by % n
    if by == 0:
        return x
    return jnp.concatenate([x[:, by:], x[:, :by]], axis=1)


def swap_pairs(count, odd, periodic):
    pairs = []
    for low in range(1 if odd else 0, count, 2):
        high = low + 1
        if high >= count:
            if not periodic:
                continue
            high = 0
        pairs += [(low, high), (high, low)]
    return pairs


def stem_kernel(fields, w_in, stem, strip_x, strip_y, tall):
    samples, variables, height, breadth = fields.shape
    odd = lax.axis_index("lon") % 2
    for b in range(samples):
        tall[b] = fields[b].astype(F32)
        cols = []
        for i in range(height):
            cols.append(tall[b, :, i, :].astype(BF))
        picked = jnp.concatenate(cols, axis=1)
        full = gelu(dot(w_in[...], picked)).astype(BF)
        stem[b] = full
        left = jnp.concatenate([full[:, i * breadth : i * breadth + HALO] for i in range(height)], axis=1)
        right = jnp.concatenate(
            [full[:, (i + 1) * breadth - HALO : (i + 1) * breadth] for i in range(height)], axis=1
        )
        strip_x[b] = jnp.where(odd == 1, left, right)
        strip_y[b] = jnp.where(odd == 1, right, left)


def widen_kernel(breadth, stem, recv_x, recv_y, half_x, half_y):
    samples = stem.shape[0]
    height = stem.shape[2] // breadth
    half = height // 2
    lon_odd = lax.axis_index("lon") % 2
    lat_odd = lax.axis_index("lat") % 2
    for b in range(samples):
        full = stem[b]
        from_x, from_y = recv_x[b], recv_y[b]
        left = jnp.where(lon_odd == 1, from_x, from_y)
        right = jnp.where(lon_odd == 1, from_y, from_x)
        halves = []
        for first in (0, half):
            pieces = []
            for m in range(4):
                for k in range(half // 4):
                    i = first + 4 * k + m
                    pieces += [
                        left[:, i * HALO : (i + 1) * HALO],
                        full[:, i * breadth : (i + 1) * breadth],
                        right[:, i * HALO : (i + 1) * HALO],
                    ]
            halves.append(jnp.concatenate(pieces, axis=1))
        half_x[b] = jnp.where(lat_odd == 1, halves[0], halves[1])
        half_y[b] = jnp.where(lat_odd == 1, halves[1], halves[0])


def unet_kernel(
    which, per_section, lat_count, breadth, plan, own_x, own_y, recv_x, recv_y, w_enc, w_down, w_mid, w_up, w_unite,
    merged, quads, zz1, zz2, zz3, zz4, sems,
):
    pitch = breadth + 2 * HALO
    lat = lax.axis_index("lat")
    section = lax.axis_index("section")
    odd = lat % 2
    first_turn = plan[0] - per_section
    last_turn = plan[2 * per_section - 1]
    sample = jnp.where(section == 0, last_turn, first_turn)
    if which == 1:
        sample = 1 - sample
    copies = []
    for n, (source, slot) in enumerate(
        ((own_x, 2 - odd), (own_y, 1 + odd), (recv_x, 3 - 3 * odd), (recv_y, 3 * odd))
    ):
        copy = pltpu.make_async_copy(source.at[sample], quads.at[slot], sems.at[n])
        copy.start()
        copies.append(copy)
    for copy in copies:
        copy.wait()
    c0 = quads.shape[1]
    lanes = quads.shape[2]
    quarter = lanes // 4
    low_edge = lat == 0
    high_edge = lat == lat_count - 1

    def keep(width, low, high):
        lane = lax.broadcasted_iota(jnp.int32, (1, width), 1)
        drop = (low_edge & (lane < low)) | (high_edge & (lane >= high))
        return jnp.where(drop, 0.0, 1.0).astype(F32)

    full_keep = keep(lanes, quarter, lanes - quarter)
    planes = [
        jnp.concatenate([quads[s, :, m * quarter : (m + 1) * quarter] for s in range(4)], axis=1)
        for m in range(4)
    ]
    rows = [shift(planes[3], -pitch)] + planes + [shift(planes[0], pitch)]
    for j, row in enumerate(rows):
        base = j * 3 * c0
        zz1[base : base + c0] = shift(row, -1)
        zz1[base + c0 : base + 2 * c0] = row
        zz1[base + 2 * c0 : base + 3 * c0] = shift(row, 1)
    skip = []
    for q in range(2):
        out = dot(w_enc[...], zz1[2 * q * 3 * c0 : (2 * q + 4) * 3 * c0])
        out = (gelu(out) * full_keep).astype(BF)
        skip += [out[:c0], out[c0:]]

    blocks = -(-lanes // 256)
    spare = blocks * 256 - lanes
    to_lane = lax.broadcasted_iota(jnp.int32, (512, 128), 1)
    from_lane = lax.broadcasted_iota(jnp.int32, (512, 128), 0) % 256
    gather = jnp.where(from_lane // 2 == to_lane, 0.25, 0.0).astype(BF)
    stacked = []
    for h in range(2):
        pair = [
            jnp.concatenate([skip[2 * h + e], jnp.zeros((c0, spare), BF)], axis=1) if spare else skip[2 * h + e]
            for e in range(2)
        ]
        for t in range(blocks):
            stacked.append(
                jnp.concatenate([pair[0][:, 256 * t : 256 * (t + 1)], pair[1][:, 256 * t : 256 * (t + 1)]], axis=1)
            )
    small = dot(jnp.concatenate(stacked, axis=0), gather).astype(BF)
    pooled = [
        jnp.concatenate([small[(h * blocks + t) * c0 : (h * blocks + t + 1) * c0] for t in range(blocks)], axis=1)
        for h in range(2)
    ]
    half_lanes = 128 * blocks
    half_pitch = pitch // 2
    half_keep = keep(half_lanes, quarter // 2, (lanes - quarter) // 2)

    def halves(scratch, source):
        width = source[0].shape[0]
        for j, row in enumerate(
            (shift(source[1], -half_pitch), source[0], source[1], shift(source[0], half_pitch))
        ):
            base = j * 3 * width
            scratch[base : base + width] = shift(row, -1)
            scratch[base + width : base + 2 * width] = row
            scratch[base + 2 * width : base + 3 * width] = shift(row, 1)

    halves(zz2, pooled)
    deep = []
    for h in range(2):
        out = dot(w_down[...], zz2[h * 3 * c0 : (h + 3) * 3 * c0])
        deep.append((gelu(out) * half_keep).astype(BF))
    halves(zz3, deep)
    c1 = deep[0].shape[0]
    lifted = []
    for h in range(2):
        out = dot(w_mid[...], zz3[h * 3 * c1 : (h + 3) * 3 * c1])
        middle = (gelu(out) + deep[h].astype(F32)).astype(BF)
        lifted.append((dot(w_up[...], middle) * half_keep).astype(BF))
    wide_lane = lax.broadcasted_iota(jnp.int32, (128, 256), 1)
    thin_lane = lax.broadcasted_iota(jnp.int32, (128, 256), 0)
    spread = jnp.where(wide_lane // 2 == thin_lane, 1.0, 0.0).astype(BF)
    stacked = jnp.concatenate(
        [lifted[h][:, 128 * t : 128 * (t + 1)] for h in range(2) for t in range(blocks)], axis=0
    )
    large = dot(stacked, spread).astype(BF)
    raised = [
        jnp.concatenate([large[(h * blocks + t) * c0 : (h * blocks + t + 1) * c0] for t in range(blocks)], axis=1)
        for h in range(2)
    ]
    start = quarter // 128 * 128
    span = zz4.shape[1]
    lift_rows = [(raised[1], -pitch), (raised[0], 0), (raised[0], 0), (raised[1], 0), (raised[1], 0), (raised[0], pitch)]
    skip_rows = [(skip[3], -pitch)] + [(s, 0) for s in skip] + [(skip[0], pitch)]
    for j in range(6):
        for b in range(3):
            base = (3 * j + b) * 2 * c0
            row, move = lift_rows[j]
            at = start + move + b - 1
            zz4[base : base + c0] = row[:, at : at + span]
            row, move = skip_rows[j]
            zz4[base + c0 : base + 2 * c0] = row[:, at : at + span]
    joined = []
    for q in range(2):
        out = dot(w_unite[...], zz4[2 * q * 6 * c0 : (2 * q + 4) * 6 * c0])
        out = gelu(out).astype(BF)
        joined += [out[:c0], out[c0:]]
    rest = quarter - start
    pieces = []
    for k in range(lanes // pitch // 2):
        for m in range(4):
            at = rest + k * pitch + HALO
            pieces.append(joined[m][:, at : at + breadth])
    merged[...] = jnp.concatenate(pieces, axis=1)


def project_kernel(per_section, map_a, map_b, w_out, out, tall):
    section = lax.axis_index("section")
    height, breadth = out.shape[2], out.shape[3]
    for n, source in enumerate((map_a, map_b)):
        full = dot(w_out[...], source[...])
        for i in range(height):
            tall[n, :, i, :] = full[:, i * breadth : (i + 1) * breadth]
        place = section if n == 0 else 1 - section
        out[pl.ds(place, 1)] = tall[n].astype(BF)[None]


def call(kernel, outs, scratch, args, spaces=None):
    vmem = pl.BlockSpec(memory_space=pltpu.VMEM)
    return pl.pallas_call(
        kernel,
        out_shape=outs,
        in_specs=spaces if spaces else [vmem] * len(args),
        out_specs=jax.tree.map(lambda _: vmem, outs),
        scratch_shapes=scratch,
        compiler_params=pltpu.CompilerParams(vmem_limit_bytes=56 << 20),
    )(*args)


def shards(fields_in, plan, in_proj, enc_conv, down_conv, mid_conv, up_proj, unite_conv, out_proj):
    samples, variables, height, breadth = fields_in.shape
    c0, c1 = in_proj.shape[0], up_proj.shape[1]
    sections, lats, lons = lax.axis_size("section"), lax.axis_size("lat"), lax.axis_size("lon")
    shape = jax.ShapeDtypeStruct
    pitch = breadth + 2 * HALO
    lanes = height // 2 * pitch

    def by_row(kernel):
        return kernel.transpose(1, 0, 2).reshape(kernel.shape[1], -1)

    def paired(kernel):
        flat = by_row(kernel)
        third = flat.shape[1] // 3
        return jnp.concatenate([jnp.pad(flat, ((0, 0), (0, third))), jnp.pad(flat, ((0, 0), (third, 0)))], axis=0)

    w_enc, w_unite = paired(enc_conv), paired(unite_conv)
    w_down, w_mid = by_row(down_conv), by_row(mid_conv)

    strip = shape((samples, c0, height * HALO), BF)
    stem, strip_x, strip_y = call(
        stem_kernel,
        (shape((samples, c0, height * breadth), BF), strip, strip),
        [pltpu.VMEM((samples, variables, height, breadth), F32)],
        (fields_in, in_proj),
    )
    recv_x = lax.ppermute(strip_x, "lon", swap_pairs(lons, False, True))
    recv_y = lax.ppermute(strip_y, "lon", swap_pairs(lons, True, True))
    half = shape((samples, c0, lanes), BF)
    half_x, half_y = call(
        lambda *refs: widen_kernel(breadth, *refs), (half, half), [], (stem, recv_x, recv_y)
    )
    far_x = lax.ppermute(half_x, "lat", swap_pairs(lats, False, False))
    far_y = lax.ppermute(half_y, "lat", swap_pairs(lats, True, False))
    hbm, vmem, smem = (pl.BlockSpec(memory_space=s) for s in (pl.ANY, pltpu.VMEM, pltpu.SMEM))
    half_lanes = -(-lanes // 256) * 128
    span = -(-(3 * (lanes // 4)) // 128) * 128 - lanes // 4 // 128 * 128

    def unet(which):
        return call(
            lambda *refs: unet_kernel(which, samples, lats, breadth, *refs),
            shape((c0, height * breadth), BF),
            [
                pltpu.VMEM((4, c0, lanes), BF),
                pltpu.VMEM((6 * 3 * c0, lanes), BF),
                pltpu.VMEM((4 * 3 * c0, half_lanes), BF),
                pltpu.VMEM((4 * 3 * c1, half_lanes), BF),
                pltpu.VMEM((6 * 6 * c0, span), BF),
                pltpu.SemaphoreType.DMA((4,)),
            ],
            (plan, half_x, half_y, far_x, far_y, w_enc, w_down, w_mid, up_proj, w_unite),
            [smem] + [hbm] * 4 + [vmem] * 5,
        )

    across = [(0, 1), (1, 0)]
    map_a = lax.ppermute(unet(0), "section", across)
    map_b = unet(1)
    map_b = lax.cond(
        plan[samples - 1] >= samples, lambda v: lax.ppermute(v, "section", across), lambda v: v, map_b
    )
    return call(
        lambda *refs: project_kernel(samples, *refs),
        shape((samples, variables, height, breadth), BF),
        [pltpu.VMEM((2, variables, height, breadth), F32)],
        (map_a, map_b, out_proj),
    )


def solution(mesh):
    return jax.shard_map(
        shards,
        mesh=mesh,
        in_specs=(P("section", None, "lat", "lon"), P(), P(), P(), P(), P(), P(), P(), P()),
        out_specs=P("section", None, "lat", "lon"),
        check_vma=False,
    )
```

time: 158 us -> 47 us (0.30)
  waiting for transfers between devices: 65.8 us -> 4.03 us
  starting transfers between devices: 34.9 us -> 10.8 us
  Pallas kernels: 0 us -> 23.9 us
  matrix products: 22.3 us -> 0 us
  between operations: 17.8 us -> 0.78 us
  other arithmetic: 7.1 us -> 1.56 us
  local copies, waits for them, and re-layouts: 9.19 us -> 5.64 us
    ppermute x16 -> x5, waiting for transfers between devices: 39.7 us -> 4.03 us  [the longest x1 2.51 us: shards(): recv_y = lax.ppermute(strip_y, 'lon', swap_pairs(lons, True, True))]
    all_gather x1 -> x0, waiting for transfers between devices: 25.4 us -> none  [shards(): gathered = lax.all_gather(fields_in, 'section', axis=0, tiled=True)]
    ppermute x16 -> x5, starting transfers between devices: 34.9 us -> 10.8 us  [the longest x1 3.35 us: shards(): far_y = lax.ppermute(half_y, 'lat', swap_pairs(lats, True, False))]
    pallas_call x0 -> x5, Pallas kernels: none -> 23.9 us  [call(): pl.pallas_call(kernel, out_shape=outs, in_specs=spaces if spaces else [vm...]
    dot_general x37 -> x0, matrix products: 22.3 us -> none  [the longest x34 17 us: convolve(): jnp.einsum('oc,bchw->bohw', kernel[3 * offset_row + offset_col], window,...]
    concatenate x5 -> x2, other arithmetic: 4.98 us -> 1.56 us  [paired(): jnp.concatenate([jnp.pad(flat, ((0, 0), (0, third))), jnp.pad(flat, ((0,...]
    unnamed x18 -> x24, local copies, waits for them, and re-layouts: 0.25 us -> 2.95 us
    dynamic_slice x2 -> x0, local copies, waits for them, and re-layouts: 2.64 us -> none  [the longest x1 1.39 us: shards(): plan[tick_num]]
  transfers between devices with their start and end apart: 17 -> 5, of which waited for: 10 -> 2; matrix products, arithmetic and copies ran while one was open for 3% -> 11% of each run, Pallas kernels for 0% -> 15%
where the time goes in v1:
time: 47 us; the launch traced here: 46.7 us
  Pallas kernels  23.9 us (51%)
  starting transfers between devices  10.8 us (23%)
  local copies, waits for them, and re-layouts  5.64 us (12%)
  waiting for transfers between devices  4.03 us (9%)
  other arithmetic  1.56 us (3%)
  between operations  0.78 us (2%)
    pallas_call x5, Pallas kernels, call(): pl.pallas_call(kernel, out_shape=outs, in_specs=spaces if spaces else [vm...  23.9 us
    ppermute x1, starting transfers between devices, shards(): far_y = lax.ppermute(half_y, 'lat', swap_pairs(lats, True, False))  3.35 us
    unnamed x24, local copies, waits for them, and re-layouts  2.95 us
    ppermute x1, waiting for transfers between devices, shards(): recv_y = lax.ppermute(strip_y, 'lon', swap_pairs(lons, True, True))  2.51 us
    ppermute x1, starting transfers between devices, shards(): recv_y = lax.ppermute(strip_y, 'lon', swap_pairs(lons, True, True))  2.2 us
    ppermute x1, starting transfers between devices, shards(): recv_x = lax.ppermute(strip_x, 'lon', swap_pairs(lons, False, True))  2.11 us
    reshape x4, local copies, waits for them, and re-layouts, by_row(): return kernel.transpose(1, 0, 2).reshape(kernel.shape[1], -1)  1.88 us
    ppermute x1, starting transfers between devices, shards(): far_x = lax.ppermute(half_x, 'lat', swap_pairs(lats, False, False))  1.82 us
  transfers between devices with their start and end apart: 5, of which 2 were waited for; matrix products, arithmetic and copies ran while one was open for 11% of the time, Pallas kernels for 15%

profile of v1, /device:TPU:1, one launch (start us, length us, event | category | flops | bytes accessed | tf_op | source)
XLA Modules:
  0.0 46.7 jit_solution(1934344421039299644)
XLA Ops:
  0.0 0.0 copy-start
  0.0 4.0 %shard_map.91 = (bf16[2,64,2048]{2,1,0:T(8,128)(2,1)}, bf16[2,64,128]{2,1,0:T(8,128)(2,1)}, bf16[2,64,128]{2,1,0:T(8,128)(2,1)}) custom-call(bf16[2,96,16,128]{3,2,1,0:T(8,128)(2,1)} %fields.1, bf16[64,96]{1,0:T(8,128)(2,1)} %w_in.1), custom_call_target="tpu_custom_call" | custom-call | tf_op jit(solution)/shard_map/pallas_call | solution.py:235
  4.1 2.1 %collective-permute-start.1 = (bf16[2,64,128]{2,1,0:T(8,128)(2,1)}, bf16[2,64,128]{2,1,0:T(8,128)(2,1)S(1)}, u32[]{:S(2)}, u32[]{:S(2)}) collective-permute-start(bf16[2,64,128]{2,1,0:T(8,128)(2,1)} %get-tuple-element.16), channel_id=1, source_target_pairs={{0,1},{1,0},{2,3},{3,2},{4,5},{5,4},{6,7},{7,6},{8,9},{9,8},{10,11... | collective-permute-start | bytes 98312 | tf_op jit(solution)/shard_map/ppermute | solution.py:271
  6.2 0.0 copy-start.5
  6.2 2.2 %collective-permute-start.2 = (bf16[2,64,128]{2,1,0:T(8,128)(2,1)}, bf16[2,64,128]{2,1,0:T(8,128)(2,1)S(1)}, u32[]{:S(2)}, u32[]{:S(2)}) collective-permute-start(bf16[2,64,128]{2,1,0:T(8,128)(2,1)} %get-tuple-element.17), channel_id=1, source_target_pairs={{1,2},{2,1},{3,0},{0,3},{5,6},{6,5},{7,4},{4,7},{9,10},{10,9},{11,... | collective-permute-start | bytes 98312 | tf_op jit(solution)/shard_map/ppermute | solution.py:272
  8.4 0.0 copy-done
  8.4 0.0 copy-done.5
  8.4 0.1 copy.15
  8.5 0.1 copy.16
  8.7 0.0 collective-permute-done.1.refs_1_
  8.7 0.0 copy-start.7
  8.7 2.5 %collective-permute-done.2.refs_2_ = bf16[2,64,128]{2,1,0:T(8,128)(2,1)S(1)} collective-permute-done((bf16[2,64,128]{2,1,0:T(8,128)(2,1)}, bf16[2,64,128]{2,1,0:T(8,128)(2,1)S(1)}, u32[]{:S(2)}, u32[]{:S(2)}) %collective-permute-start.2) | collective-permute-done | bytes 32800 | tf_op jit(solution)/shard_map/ppermute | solution.py:272
  11.2 0.0 copy-start.8
  11.2 0.0 copy-done.7
  11.2 0.6 %copy-done.8 = bf16[2,64,128]{2,1,0:T(8,128)(2,1)} copy-done((bf16[2,64,128]{2,1,0:T(8,128)(2,1)}, bf16[2,64,128]{2,1,0:T(8,128)(2,1)S(1)}, u32[]{:S(2)}) %copy-start.8) | copy-done | bytes 32792
  11.8 2.3 %shard_map.92 = (bf16[2,64,1152]{2,1,0:T(8,128)(2,1)}, bf16[2,64,1152]{2,1,0:T(8,128)(2,1)}) custom-call(bf16[2,64,2048]{2,1,0:T(8,128)(2,1)} %get-tuple-element.15.refs_0_, bf16[2,64,128]{2,1,0:T(8,128)(2,1)} %copy-done.7, bf16[2,64,128]{2,1,0:T(8,128)(2,1)} %copy-done.8), custom_call_target="tpu_custom_call" | custom-call | tf_op jit(solution)/shard_map/pallas_call | solution.py:235
  14.1 0.0 copy-start.6
  14.1 1.8 %collective-permute-start.3 = (bf16[2,64,1152]{2,1,0:T(8,128)(2,1)}, bf16[2,64,1152]{2,1,0:T(8,128)(2,1)S(1)}, u32[]{:S(2)}, u32[]{:S(2)}) collective-permute-start(bf16[2,64,1152]{2,1,0:T(8,128)(2,1)} %get-tuple-element.18.refs_1_), channel_id=1, source_target_pairs={{0,4},{4,0},{8,12},{12,8},{1,5},{5,1},{9,13},{13,9},{2,6},{6,2},{1... | collective-permute-start | bytes 884744 | tf_op jit(solution)/shard_map/ppermute | solution.py:277
  15.9 0.0 copy-start.3
  15.9 3.4 %collective-permute-start.4 = (bf16[2,64,1152]{2,1,0:T(8,128)(2,1)}, bf16[2,64,1152]{2,1,0:T(8,128)(2,1)S(1)}, u32[]{:S(2)}, u32[]{:S(2)}) collective-permute-start(bf16[2,64,1152]{2,1,0:T(8,128)(2,1)} %get-tuple-element.19.refs_2_), channel_id=1, source_target_pairs={{4,8},{8,4},{5,9},{9,5},{6,10},{10,6},{7,11},{11,7},{20,24},{24,20... | collective-permute-start | bytes 884744 | tf_op jit(solution)/shard_map/ppermute | solution.py:278
  19.3 0.8 %fusion.5.refs_5_ = bf16[128,768]{1,0:T(8,128)(2,1)} fusion(bf16[64,576]{1,0:T(8,128)(2,1)S(1)} %copy.16), kind=kLoop, calls=%fused_computation.9 | loop fusion | flops 786432 | bytes 270336 | tf_op jit(solution)/shard_map/concatenate | solution.py:259
  20.1 0.0 copy-done.6
  20.1 0.8 %copy.20.refs_6_ = bf16[128,576]{1,0:T(8,128)(2,1)} copy(bf16[128,576]{0,1:T(8,128)(2,1)S(1)} %bitcast.18) | data formatting | bytes 294912 | tf_op jit(solution)/shard_map/reshape | solution.py:254
  20.9 0.0 copy-done.3
  20.9 0.2 copy.18
  21.1 0.9 %copy.21.refs_7_ = bf16[128,1152]{1,0:T(8,128)(2,1)} copy(bf16[128,1152]{0,1:T(8,128)(2,1)S(1)} %bitcast.15) | data formatting | bytes 589824 | tf_op jit(solution)/shard_map/reshape | solution.py:254
  22.0 0.8 %fusion.2.refs_9_ = bf16[128,1536]{1,0:T(8,128)(2,1)} fusion(bf16[64,1152]{1,0:T(8,128)(2,1)S(1)} %copy_bitcast_fusion), kind=kLoop, calls=%fused_computation.4 | loop fusion | flops 1572864 | bytes 540672 | tf_op jit(solution)/shard_map/concatenate | solution.py:259
  22.8 0.0 copy-start.10
  22.8 0.0 collective-permute-done.3.refs_3_
  22.8 0.0 copy-start.1
  22.8 1.5 %collective-permute-done.4.refs_4_ = bf16[2,64,1152]{2,1,0:T(8,128)(2,1)S(1)} collective-permute-done((bf16[2,64,1152]{2,1,0:T(8,128)(2,1)}, bf16[2,64,1152]{2,1,0:T(8,128)(2,1)S(1)}, u32[]{:S(2)}, u32[]{:S(2)}) %collective-permute-start.4) | collective-permute-done | bytes 294944 | tf_op jit(solution)/shard_map/ppermute | solution.py:278
  24.3 0.0 copy-done.1
  24.3 0.0 copy-start.2
  24.3 0.7 %copy-done.2 = bf16[2,64,1152]{2,1,0:T(8,128)(2,1)} copy-done((bf16[2,64,1152]{2,1,0:T(8,128)(2,1)}, bf16[2,64,1152]{2,1,0:T(8,128)(2,1)S(1)}, u32[]{:S(2)}) %copy-start.2) | copy-done | bytes 294936
  25.0 0.0 copy-start.9
  25.0 7.7 %shard_map.93 = bf16[64,2048]{1,0:T(8,128)(2,1)} custom-call(s32[4]{0:T(128)} %refs_0_.3, bf16[2,64,1152]{2,1,0:T(8,128)(2,1)} %get-tuple-element.18.refs_1_, bf16[2,64,1152]{2,1,0:T(8,128)(2,1)} %get-tuple-element.19.refs_2_, bf16[2,64,1152]{2,1,0:T(8,128)(2,1)} %copy-done.1, bf16[2,64,1152]{2,1,0:T(8,128)(2,1)} %copy-done.2, ...), custom_call_target="tpu_custom_call" | custom-call | tf_op jit(solution)/shard_map/pallas_call | solution.py:235
  32.7 1.3 %collective-permute-start.5 = (bf16[64,2048]{1,0:T(8,128)(2,1)}, bf16[64,2048]{1,0:T(8,128)(2,1)S(1)}, u32[]{:S(2)}, u32[]{:S(2)}) collective-permute-start(bf16[64,2048]{1,0:T(8,128)(2,1)} %shard_map.93), channel_id=1, source_target_pairs={{0,16},{16,0},{1,17},{17,1},{2,18},{18,2},{3,19},{19,3},{4,20},{20... | collective-permute-start | bytes 786440 | tf_op jit(solution)/shard_map/ppermute | solution.py:300
  34.0 0.0 copy-done.10
  34.0 0.7 %slice.3 = s32[1]{0:T(128)} slice(s32[4]{0:T(128)S(1)} %copy-done.10), slice={[1:2]} | slice | bytes 8 | tf_op jit(solution)/shard_map/slice | solution.py:303
  35.3 0.0 copy-done.9
  35.4 0.7 %copy.24.refs_2_ = bf16[96,64]{1,0:T(8,128)(2,1)} copy(bf16[96,64]{0,1:T(8,128)(2,1)S(1)} %copy-done.9) | data formatting | bytes 24576 | tf_op args[8]
  36.1 7.0 %shard_map.94 = bf16[64,2048]{1,0:T(8,128)(2,1)S(1)} custom-call(s32[4]{0:T(128)} %refs_0_.3, bf16[2,64,1152]{2,1,0:T(8,128)(2,1)} %get-tuple-element.18.refs_1_, bf16[2,64,1152]{2,1,0:T(8,128)(2,1)} %get-tuple-element.19.refs_2_, bf16[2,64,1152]{2,1,0:T(8,128)(2,1)} %copy-done.1, bf16[2,64,1152]{2,1,0:T(8,128)(2,1)} %copy-done.2, ...), custom_call_target="tpu_custom_call" | custom-call | tf_op jit(solution)/shard_map/pallas_call | solution.py:235
  43.0 0.0 collective-permute-done.5.refs_0_
  43.1 0.0 copy-start.4
  43.1 0.7 %copy-done.4 = bf16[64,2048]{1,0:T(8,128)(2,1)} copy-done((bf16[64,2048]{1,0:T(8,128)(2,1)}, bf16[64,2048]{1,0:T(8,128)(2,1)S(1)}, u32[]{:S(2)}) %copy-start.4) | copy-done | bytes 262168
  43.7 3.0 %shard_map.95 = bf16[2,96,16,128]{3,2,1,0:T(8,128)(2,1)} custom-call(bf16[64,2048]{1,0:T(8,128)(2,1)} %copy-done.4, bf16[64,2048]{1,0:T(8,128)(2,1)S(1)} %get-tuple-element.20.refs_1_, bf16[96,64]{1,0:T(8,128)(2,1)} %copy.24.refs_2_), custom_call_target="tpu_custom_call" | custom-call | tf_op jit(solution)/shard_map/pallas_call | solution.py:235
  (2 shorter events, 0.0 us)
Async XLA Ops:
  0.0 8.4 %copy-start = (bf16[9,64,128]{2,1,0:T(8,128)(2,1)S(1)}, bf16[9,64,128]{2,1,0:T(8,128)(2,1)}, u32[]{:S(2)}) copy-start(bf16[9,64,128]{2,1,0:T(8,128)(2,1)} %param.18) | copy-start | bytes 442372
  4.1 4.6 %collective-permute-start.1 = (bf16[2,64,128]{2,1,0:T(8,128)(2,1)}, bf16[2,64,128]{2,1,0:T(8,128)(2,1)S(1)}, u32[]{:S(2)}, u32[]{:S(2)}) collective-permute-start(bf16[2,64,128]{2,1,0:T(8,128)(2,1)} %get-tuple-element.16), channel_id=1, source_target_pairs={{0,1},{1,0},{2,3},{3,2},{4,5},{5,4},{6,7},{7,6},{8,9},{9,8},{10,11... | collective-permute-start | bytes 98312 | tf_op jit(solution)/shard_map/ppermute | solution.py:271
  6.2 2.2 %copy-start.5 = (bf16[9,64,64]{2,1,0:T(8,128)(2,1)S(1)}, bf16[9,64,64]{2,1,0:T(8,128)(2,1)}, u32[]{:S(2)}) copy-start(bf16[9,64,64]{2,1,0:T(8,128)(2,1)} %param.14) | copy-start | bytes 221188
  6.2 5.1 %collective-permute-start.2 = (bf16[2,64,128]{2,1,0:T(8,128)(2,1)}, bf16[2,64,128]{2,1,0:T(8,128)(2,1)S(1)}, u32[]{:S(2)}, u32[]{:S(2)}) collective-permute-start(bf16[2,64,128]{2,1,0:T(8,128)(2,1)} %get-tuple-element.17), channel_id=1, source_target_pairs={{1,2},{2,1},{3,0},{0,3},{5,6},{6,5},{7,4},{4,7},{9,10},{10,9},{11,... | collective-permute-start | bytes 98312 | tf_op jit(solution)/shard_map/ppermute | solution.py:272
  8.7 2.5 %copy-start.7 = (bf16[2,64,128]{2,1,0:T(8,128)(2,1)}, bf16[2,64,128]{2,1,0:T(8,128)(2,1)S(1)}, u32[]{:S(2)}) copy-start(bf16[2,64,128]{2,1,0:T(8,128)(2,1)S(1)} %collective-permute-done.1.refs_1_) | copy-start | bytes 98308
  11.2 0.6 %copy-start.8 = (bf16[2,64,128]{2,1,0:T(8,128)(2,1)}, bf16[2,64,128]{2,1,0:T(8,128)(2,1)S(1)}, u32[]{:S(2)}) copy-start(bf16[2,64,128]{2,1,0:T(8,128)(2,1)S(1)} %collective-permute-done.2.refs_2_) | copy-start | bytes 98308
  14.1 6.0 %copy-start.6 = (bf16[9,128,64]{1,2,0:T(8,128)(2,1)S(1)}, bf16[9,128,64]{1,2,0:T(8,128)(2,1)}, u32[]{:S(2)}) copy-start(bf16[9,128,64]{1,2,0:T(8,128)(2,1)} %param.15) | copy-start | bytes 442372
  14.1 8.7 %collective-permute-start.3 = (bf16[2,64,1152]{2,1,0:T(8,128)(2,1)}, bf16[2,64,1152]{2,1,0:T(8,128)(2,1)S(1)}, u32[]{:S(2)}, u32[]{:S(2)}) collective-permute-start(bf16[2,64,1152]{2,1,0:T(8,128)(2,1)} %get-tuple-element.18.refs_1_), channel_id=1, source_target_pairs={{0,4},{4,0},{8,12},{12,8},{1,5},{5,1},{9,13},{13,9},{2,6},{6,2},{1... | collective-permute-start | bytes 884744 | tf_op jit(solution)/shard_map/ppermute | solution.py:277
  15.9 5.0 %copy-start.3 = (bf16[9,128,128]{2,1,0:T(8,128)(2,1)S(1)}, bf16[9,128,128]{2,1,0:T(8,128)(2,1)}, u32[]{:S(2)}) copy-start(bf16[9,128,128]{2,1,0:T(8,128)(2,1)} %param.16) | copy-start | bytes 884740
  15.9 8.4 %collective-permute-start.4 = (bf16[2,64,1152]{2,1,0:T(8,128)(2,1)}, bf16[2,64,1152]{2,1,0:T(8,128)(2,1)S(1)}, u32[]{:S(2)}, u32[]{:S(2)}) collective-permute-start(bf16[2,64,1152]{2,1,0:T(8,128)(2,1)} %get-tuple-element.19.refs_2_), channel_id=1, source_target_pairs={{4,8},{8,4},{5,9},{9,5},{6,10},{10,6},{7,11},{11,7},{20,24},{24,20... | collective-permute-start | bytes 884744 | tf_op jit(solution)/shard_map/ppermute | solution.py:278
  22.8 11.2 %copy-start.10 = (s32[4]{0:T(128)S(1)}, s32[4]{0:T(128)}, u32[]{:S(2)}) copy-start(s32[4]{0:T(128)} %refs_0_.3) | copy-start | bytes 52
  22.8 1.5 %copy-start.1 = (bf16[2,64,1152]{2,1,0:T(8,128)(2,1)}, bf16[2,64,1152]{2,1,0:T(8,128)(2,1)S(1)}, u32[]{:S(2)}) copy-start(bf16[2,64,1152]{2,1,0:T(8,128)(2,1)S(1)} %collective-permute-done.3.refs_3_) | copy-start | bytes 884740
  24.3 0.7 %copy-start.2 = (bf16[2,64,1152]{2,1,0:T(8,128)(2,1)}, bf16[2,64,1152]{2,1,0:T(8,128)(2,1)S(1)}, u32[]{:S(2)}) copy-start(bf16[2,64,1152]{2,1,0:T(8,128)(2,1)S(1)} %collective-permute-done.4.refs_4_) | copy-start | bytes 884740
  25.0 10.3 %copy-start.9 = (bf16[96,64]{0,1:T(8,128)(2,1)S(1)}, bf16[96,64]{0,1:T(8,128)(2,1)}, u32[]{:S(2)}) copy-start(bf16[96,64]{0,1:T(8,128)(2,1)} %param.19) | copy-start | bytes 36868
  32.7 10.3 %collective-permute-start.5 = (bf16[64,2048]{1,0:T(8,128)(2,1)}, bf16[64,2048]{1,0:T(8,128)(2,1)S(1)}, u32[]{:S(2)}, u32[]{:S(2)}) collective-permute-start(bf16[64,2048]{1,0:T(8,128)(2,1)} %shard_map.93), channel_id=1, source_target_pairs={{0,16},{16,0},{1,17},{17,1},{2,18},{18,2},{3,19},{19,3},{4,20},{20... | collective-permute-start | bytes 786440 | tf_op jit(solution)/shard_map/ppermute | solution.py:300
  43.1 0.7 %copy-start.4 = (bf16[64,2048]{1,0:T(8,128)(2,1)}, bf16[64,2048]{1,0:T(8,128)(2,1)S(1)}, u32[]{:S(2)}) copy-start(bf16[64,2048]{1,0:T(8,128)(2,1)S(1)} %collective-permute-done.5.refs_0_) | copy-start | bytes 786436
